TPU v7x, 128 devices: a whole 4x4x4 slice. The times are simulated.
128 devices in a mesh: lat: 16 (over x, z_lo, core), lon: 8 (over z_hi, y).
Axes of the slice: x: 4, y: 4, z: 4 (z_hi: 2, z_lo: 2; z = z_hi * 2 + z_lo), core: 2. Of those that a mesh axis runs over, the one named last changes fastest.
Arguments:
- current: bfloat16 [69, 512, 1024], P(None, 'lat', 'lon')
- next_fields: bfloat16 [128, 512, 1024], P(('lat', 'lon')), may hold values from -6 to 6
- reader_slot: int32 [69], replicated, may hold values from 0 to 127, as said below
- first_weight: bfloat16 [9, 256, 69], replicated, may hold values from -0.25 to 0.25
- first_bias: float32 [256], replicated, may hold values from -3 to 3
- second_weight: bfloat16 [9, 256, 256], replicated, may hold values from -0.125 to 0.125
- second_bias: float32 [256], replicated, may hold values from -3 to 3
Outputs:
- features: bfloat16 [256, 512, 1024], P(None, 'lat', 'lon')
- next_tile: bfloat16 [69, 512, 1024], P(None, 'lat', 'lon')
Inputs may be any that keep to these rules, and one draw needn't show every extreme that they name: `reader_slot`: the 69 entries are different slots.
All inputs are finite; a program needn't handle non-finite values.
Results may differ from a plain program's by a relative error of at most 0.0053.
Values may be sent and summed in bfloat16 or wider, within the bound.
A program may use at most 128 MiB of HBM per device.

v0:
```python
import functools

import jax
import jax.numpy as jnp
from jax import lax
from jax.sharding import Mesh
from jax.sharding import PartitionSpec as P

LAT = ("lat_0", "lat_1", "lat_2")
LON = ("lon_0", "lon_1")
LAT_LON = ("lat_0", "lat_1", "lat_2", "lon_0", "lon_1")


def one_axis_at_a_time(array, axes):
    return functools.reduce(lax.psum, axes, array)


def padded_2(block, sides, width, periodic):
    for axis, dim in sides:
        count = lax.axis_size(axis)
        forward = [(i, i + 1) for i in range(count - 1)]
        if periodic:
            forward.append((count - 1, 0))
        backward = [(target, source) for source, target in forward]
        low = lax.ppermute(
            lax.slice_in_dim(block, block.shape[dim] - width, None, axis=dim), axis, forward
        )
        high = lax.ppermute(lax.slice_in_dim(block, 0, width, axis=dim), axis, backward)
        block = jnp.concatenate([low, block, high], axis=dim)
    return block


def conv_valid(padded, weight, bias):
    rows = padded.shape[1] - 2
    cols = padded.shape[2] - 2
    total = jnp.zeros((weight.shape[1], rows, cols), jnp.float32)
    for tap in range(9):
        shifted = padded[:, tap // 3 : tap // 3 + rows, tap % 3 : tap % 3 + cols]
        total = total + jnp.einsum(
            "ok,khw->ohw", weight[tap], shifted, preferred_element_type=jnp.float32
        )
    return total + bias[:, None, None]


def regrid(next_fields, reader_slot):
    slot_dev, rows_all, cols_all = next_fields.shape
    n_lat = lax.axis_size(LAT)
    n_lon = lax.axis_size(LON)
    lat_rows = rows_all // n_lat
    lon_cols = cols_all // n_lon
    blocks = next_fields.reshape(slot_dev, n_lat, lat_rows, n_lon, lon_cols)
    ordered = blocks.transpose(1, 3, 0, 2, 4).reshape(n_lat * n_lon, slot_dev, lat_rows, lon_cols)
    moved = lax.all_to_all(ordered, LAT_LON, split_axis=0, concat_axis=1, tiled=True)
    moved = moved.reshape(n_lat * n_lon * slot_dev, lat_rows, lon_cols)
    return jnp.take(moved, reader_slot, axis=0)


def encode(current, first_weight, first_bias, second_weight, second_bias):
    values = current.astype(jnp.float32)
    lat_rows = values.shape[1]
    lon_cols = values.shape[2]
    cells = lat_rows * lax.axis_size(LAT) * lon_cols * lax.axis_size(LON)
    total, squares = (
        one_axis_at_a_time(jnp.sum(values, axis=(1, 2)), LAT_LON),
        one_axis_at_a_time(jnp.sum(values * values, axis=(1, 2)), LAT_LON),
    )
    mean = total / cells
    scale = 1.0 / jnp.sqrt(squares / cells - mean * mean + 1e-05)
    normed = ((values - mean[:, None, None]) * scale[:, None, None]).astype(jnp.bfloat16)
    tall = padded_2(normed, ((LAT, 1),), 2, False)
    padded = padded_2(tall, ((LON, 2),), 2, True)
    hidden = jax.nn.gelu(conv_valid(padded, first_weight, first_bias), approximate=True)
    global_row = lax.axis_index(LAT) * lat_rows + jnp.arange(lat_rows + 2, dtype=jnp.int32) - 1
    inside = (global_row >= 0) & (global_row < lat_rows * lax.axis_size(LAT))
    hidden = jnp.where(inside[None, :, None], hidden, 0.0).astype(jnp.bfloat16)
    return conv_valid(hidden, second_weight, second_bias).astype(jnp.bfloat16)


def body(current, next_fields, reader_slot, first_weight, first_bias, second_weight, second_bias):
    features = encode(current, first_weight, first_bias, second_weight, second_bias)
    next_tile = regrid(next_fields, reader_slot)
    return (features, next_tile)


def solution(mesh):
    split = Mesh(mesh.devices.reshape(4, 2, 2, 2, 4), ("lat_0", "lat_1", "lat_2", "lon_0", "lon_1"))
    return jax.shard_map(
        body,
        mesh=split,
        in_specs=(P(None, LAT, LON), P(LAT_LON, None, None), P(), P(), P(), P(), P()),
        out_specs=(P(None, LAT, LON), P(None, LAT, LON)),
        check_vma=False,
    )
```

profile of v0, /device:TPU:4, one launch (start us, length us, event | category | flops | bytes accessed | tf_op | source)
XLA Modules:
  0.0 140.9 jit_solution(8600017276479272520)
XLA Ops:
  3.1 8.3 %all-reduce.1 = (f32[69]{0:T(128)S(1)}, f32[69]{0:T(128)S(1)}) all-reduce(f32[69]{0:T(128)S(1)} %get-tuple-element.11, f32[69]{0:T(128)S(1)} %get-tuple-element.10), channel_id=1, replica_groups=mesh['lat_0'=4,'lat_1'=2,'lat_2'=2,'lon_0'=2,'lon_1'=4] {'lat_0'}, use_global_device_ids=true, to_apply=%region_7.0 | all-reduce | flops 138 | bytes 1104 | tf_op jit(solution)/shard_map/psum | solution.py:15
  11.4 4.9 %all-reduce.4 = (f32[69]{0:T(128)S(1)}, f32[69]{0:T(128)S(1)}) all-reduce(f32[69]{0:T(128)S(1)} %get-tuple-element.14, f32[69]{0:T(128)S(1)} %get-tuple-element.15), channel_id=1, replica_groups=mesh['lat_0'=4,'lat_1'=2,'lat_2'=2,'lon_0'=2,'lon_1'=4] {'lat_1'}, use_global_device_ids=true, to_apply=%region_8.0 | all-reduce | flops 138 | bytes 1104 | tf_op jit(solution)/shard_map/psum | solution.py:15
  18.8 6.8 %all-reduce.2 = (f32[69]{0:T(128)S(1)}, f32[69]{0:T(128)S(1)}) all-reduce(f32[69]{0:T(128)S(1)} %get-tuple-element.18, f32[69]{0:T(128)S(1)} %get-tuple-element.19), channel_id=1, replica_groups=mesh['lat_0'=4,'lat_1'=2,'lat_2'=2,'lon_0'=2,'lon_1'=4] {'lon_0'}, use_global_device_ids=true, to_apply=%region_10.0 | all-reduce | flops 138 | bytes 1104 | tf_op jit(solution)/shard_map/psum | solution.py:15
  25.5 10.7 %all-reduce = (f32[69]{0:T(128)S(1)}, f32[69]{0:T(128)S(1)}) all-reduce(f32[69]{0:T(128)S(1)} %get-tuple-element.16, f32[69]{0:T(128)S(1)} %get-tuple-element.17), channel_id=1, replica_groups=mesh['lat_0'=4,'lat_1'=2,'lat_2'=2,'lon_0'=2,'lon_1'=4] {'lon_1'}, use_global_device_ids=true, to_apply=%region_11.0 | all-reduce | flops 138 | bytes 1104 | tf_op jit(solution)/shard_map/psum | solution.py:15
  38.5 4.5 %collective-permute-start.1 = (bf16[69,2,128]{0,2,1:T(8,128)(2,1)S(1)}, bf16[69,2,128]{0,2,1:T(8,128)(2,1)S(1)}, u32[]{:S(2)}, u32[]{:S(2)}) collective-permute-start(bf16[69,2,128]{0,2,1:T(8,128)(2,1)S(1)} %get-tuple-element.25), channel_id=1, source_target_pairs={{8,0},{16,8},{24,16},{32,24},{40,32},{48,40},{56,48},{64,56},{72,6... | collective-permute-start | bytes 105992 | tf_op jit(solution)/shard_map/ppermute | solution.py:28
  44.6 8.1 %all-to-all-start = ((bf16[128,1,32,128]{3,2,1,0:T(8,128)(2,1)}), bf16[128,1,32,128]{3,2,1,0:T(8,128)(2,1)}, u32[]{:S(2)}, u32[]{:S(2)}) async-start(bf16[128,1,32,128]{3,2,1,0:T(8,128)(2,1)} %bitcast.40), calls=%async_computation | async-start | bytes 2097152 | tf_op jit(solution)/shard_map/all_to_all | solution.py:53
  52.8 5.8 %collective-permute-start.3 = (bf16[69,36,2]{0,2,1:T(2,128)(2,1)S(1)}, bf16[69,36,2]{0,2,1:T(2,128)(2,1)S(1)}, u32[]{:S(2)}, u32[]{:S(2)}) collective-permute-start(bf16[69,36,2]{0,2,1:T(2,128)(2,1)S(1)} %get-tuple-element.23), channel_id=1, source_target_pairs={{1,0},{2,1},{3,2},{4,3},{5,4},{6,5},{7,6},{0,7},{9,8},{10,9},{11,1... | collective-permute-start | bytes 29816 | tf_op jit(solution)/shard_map/ppermute | solution.py:28
  58.6 6.9 %collective-permute-done.3 = bf16[69,36,2]{0,2,1:T(2,128)(2,1)S(1)} collective-permute-done((bf16[69,36,2]{0,2,1:T(2,128)(2,1)S(1)}, bf16[69,36,2]{0,2,1:T(2,128)(2,1)S(1)}, u32[]{:S(2)}, u32[]{:S(2)}) %collective-permute-start.3) | collective-permute-done | bytes 9968 | tf_op jit(solution)/shard_map/ppermute | solution.py:28
  65.5 4.4 %collective-permute-done.2 = bf16[69,36,2]{0,2,1:T(2,128)(2,1)S(1)} collective-permute-done((bf16[69,36,2]{0,2,1:T(2,128)(2,1)S(1)}, bf16[69,36,2]{0,2,1:T(2,128)(2,1)S(1)}, u32[]{:S(2)}, u32[]{:S(2)}) %collective-permute-start.2) | collective-permute-done | bytes 9968 | tf_op jit(solution)/shard_map/ppermute | solution.py:25
  71.1 3.0 %fusion.34 = f32[34,130,256]{2,1,0:T(8,128)} fusion(bf16[69,36,132]{0,2,1:T(8,128)(2,1)S(1)} %pad_maximum_fusion, bf16[9,256,69]{1,2,0:T(8,128)(2,1)S(1)} %copy-done.2), kind=kOutput, calls=%fused_computation.41 | convolution fusion | flops 156149760 | bytes 5746688 | tf_op jit(solution)/shard_map/ok,khw->ohw/dot_general | solution.py:39
  74.2 2.9 %fusion.36 = f32[34,130,256]{2,1,0:T(8,128)} fusion(bf16[69,36,132]{0,2,1:T(8,128)(2,1)S(1)} %pad_maximum_fusion, bf16[9,256,69]{1,2,0:T(8,128)(2,1)S(1)} %copy-done.2), kind=kOutput, calls=%fused_computation.43 | convolution fusion | flops 156149760 | bytes 5746688 | tf_op jit(solution)/shard_map/ok,khw->ohw/dot_general | solution.py:39
  77.1 2.9 %fusion.63 = f32[34,130,256]{2,1,0:T(8,128)} fusion(bf16[9,256,69]{1,2,0:T(8,128)(2,1)S(1)} %copy-done.2, bf16[69,36,2]{0,2,1:T(2,128)(2,1)S(1)} %collective-permute-done.3, bf16[69,2,128]{0,2,1:T(8,128)(2,1)S(1)} %collective-permute-done.1, bf16[69,32,128]{0,2,1:T(8,128)(2,1)S(1)} %fusion.10, bf16[69,2,128]{0,2,1:T(8,128)(2,1)S(1)} %collective-permute-done), kind=kOutput, calls=%fused_computation.69 | convolution fusion | flops 158733120 | bytes 5761024 | tf_op jit(solution)/shard_map/ok,khw->ohw/dot_general | solution.py:39
  80.0 2.9 %fusion.66 = f32[34,130,256]{2,1,0:T(8,128)} fusion(bf16[9,256,69]{1,2,0:T(8,128)(2,1)S(1)} %copy-done.2, bf16[69,2,128]{0,2,1:T(8,128)(2,1)S(1)} %collective-permute-done.1, bf16[69,32,128]{0,2,1:T(8,128)(2,1)S(1)} %fusion.10, bf16[69,2,128]{0,2,1:T(8,128)(2,1)S(1)} %collective-permute-done, bf16[69,36,2]{0,2,1:T(2,128)(2,1)S(1)} %collective-permute-done.2), kind=kOutput, calls=%fused_computation.72 | convolution fusion | flops 158733120 | bytes 5761024 | tf_op jit(solution)/shard_map/ok,khw->ohw/dot_general | solution.py:39
  82.9 2.9 %fusion.68 = f32[34,130,256]{2,1,0:T(8,128)} fusion(bf16[9,256,69]{1,2,0:T(8,128)(2,1)S(1)} %copy-done.2, bf16[69,36,2]{0,2,1:T(2,128)(2,1)S(1)} %collective-permute-done.3, bf16[69,2,128]{0,2,1:T(8,128)(2,1)S(1)} %collective-permute-done.1, bf16[69,32,128]{0,2,1:T(8,128)(2,1)S(1)} %fusion.10, bf16[69,2,128]{0,2,1:T(8,128)(2,1)S(1)} %collective-permute-done), kind=kOutput, calls=%fused_computation.74 | convolution fusion | flops 158733120 | bytes 5761024 | tf_op jit(solution)/shard_map/ok,khw->ohw/dot_general | solution.py:39
  85.8 3.0 %fusion.71 = f32[34,130,256]{2,1,0:T(8,128)} fusion(bf16[9,256,69]{1,2,0:T(8,128)(2,1)S(1)} %copy-done.2, bf16[69,2,128]{0,2,1:T(8,128)(2,1)S(1)} %collective-permute-done.1, bf16[69,32,128]{0,2,1:T(8,128)(2,1)S(1)} %fusion.10, bf16[69,2,128]{0,2,1:T(8,128)(2,1)S(1)} %collective-permute-done, bf16[69,36,2]{0,2,1:T(2,128)(2,1)S(1)} %collective-permute-done.2), kind=kOutput, calls=%fused_computation.77 | convolution fusion | flops 158733120 | bytes 5761024 | tf_op jit(solution)/shard_map/ok,khw->ohw/dot_general | solution.py:39
  88.8 2.9 %fusion.61 = f32[34,130,256]{2,1,0:T(8,128)} fusion(bf16[9,256,69]{1,2,0:T(8,128)(2,1)S(1)} %copy-done.2, bf16[69,2,128]{0,2,1:T(8,128)(2,1)S(1)} %collective-permute-done.1, bf16[69,32,128]{0,2,1:T(8,128)(2,1)S(1)} %fusion.10, bf16[69,2,128]{0,2,1:T(8,128)(2,1)S(1)} %collective-permute-done, bf16[69,36,2]{0,2,1:T(2,128)(2,1)S(1)} %collective-permute-done.2), kind=kOutput, calls=%fused_computation.67 | convolution fusion | flops 158733120 | bytes 5761024 | tf_op jit(solution)/shard_map/ok,khw->ohw/dot_general | solution.py:39
  91.7 12.7 %fusion.8 = bf16[256,34,130]{0,2,1:T(8,128)(2,1)S(1)} fusion(f32[34,130,256]{2,1,0:T(8,128)S(1)} %fusion.32, f32[34,130,256]{2,1,0:T(8,128)} %fusion.61, f32[34,130,256]{2,1,0:T(8,128)} %fusion.63, f32[34,130,256]{2,1,0:T(8,128)} %fusion.34, f32[34,130,256]{2,1,0:T(8,128)} %fusion.66, f32[34,130,256]{2,1,0:T(8,128)} %fusion.68, ...), kind=kOutput, calls=%fused_computation.10 | convolution fusion | flops 180232000 | bytes 39917056 | tf_op jit(solution)/shard_map/ok,khw->ohw/dot_general | solution.py:39
  107.9 2.7 %fusion.17 = f32[32,128,256]{2,1,0:T(8,128)} fusion(bf16[256,34,130]{0,2,1:T(8,128)(2,1)S(1)} %fusion.8, bf16[9,256,256]{2,1,0:T(8,128)(2,1)S(1)} %copy-done), kind=kOutput, calls=%fused_computation.23 | convolution fusion | flops 536870912 | bytes 6422528 | tf_op jit(solution)/shard_map/ok,khw->ohw/dot_general | solution.py:39
  110.6 2.7 %fusion.19 = f32[32,128,256]{2,1,0:T(8,128)} fusion(bf16[256,34,130]{0,2,1:T(8,128)(2,1)S(1)} %fusion.8, bf16[9,256,256]{2,1,0:T(8,128)(2,1)S(1)} %copy-done), kind=kOutput, calls=%fused_computation.25 | convolution fusion | flops 536870912 | bytes 6422528 | tf_op jit(solution)/shard_map/ok,khw->ohw/dot_general | solution.py:39
  116.0 2.7 %fusion.23 = f32[32,128,256]{2,1,0:T(8,128)} fusion(bf16[256,34,130]{0,2,1:T(8,128)(2,1)S(1)} %fusion.8, bf16[9,256,256]{2,1,0:T(8,128)(2,1)S(1)} %copy-done), kind=kOutput, calls=%fused_computation.29 | convolution fusion | flops 536870912 | bytes 6422528 | tf_op jit(solution)/shard_map/ok,khw->ohw/dot_general | solution.py:39
  118.7 2.7 %fusion.25 = f32[32,128,256]{2,1,0:T(8,128)} fusion(bf16[256,34,130]{0,2,1:T(8,128)(2,1)S(1)} %fusion.8, bf16[9,256,256]{2,1,0:T(8,128)(2,1)S(1)} %copy-done), kind=kOutput, calls=%fused_computation.31 | convolution fusion | flops 536870912 | bytes 6422528 | tf_op jit(solution)/shard_map/ok,khw->ohw/dot_general | solution.py:39
  121.5 2.7 %fusion.27 = f32[32,128,256]{2,1,0:T(8,128)} fusion(bf16[256,34,130]{0,2,1:T(8,128)(2,1)S(1)} %fusion.8, bf16[9,256,256]{2,1,0:T(8,128)(2,1)S(1)} %copy-done), kind=kOutput, calls=%fused_computation.33 | convolution fusion | flops 536870912 | bytes 6422528 | tf_op jit(solution)/shard_map/ok,khw->ohw/dot_general | solution.py:39
  124.2 10.8 %fusion.29 = bf16[256,32,128]{0,2,1:T(8,128)(2,1)S(1)} fusion(f32[256]{0:T(256)S(1)} %copy-done.4, bf16[256,34,130]{0,2,1:T(8,128)(2,1)S(1)} %fusion.8, f32[32,128,256]{2,1,0:T(8,128)S(1)} %fusion.13, f32[32,128,256]{2,1,0:T(8,128)} %fusion.15, f32[32,128,256]{2,1,0:T(8,128)} %fusion.17, f32[32,128,256]{2,1,0:T(8,128)} %fusion.19, ...), kind=kOutput, calls=%fused_computation.35 | convolution fusion | flops 547356672 | bytes 37880832 | tf_op jit(solution)/shard_map/ok,khw->ohw/dot_general | solution.py:39
  134.9 3.1 %copy.19 = bf16[256,32,128]{2,1,0:T(8,128)(2,1)} copy(bf16[256,32,128]{0,2,1:T(8,128)(2,1)S(1)} %fusion.29) | data formatting | bytes 4194304
  (37 shorter events, 18.9 us)
Async XLA Ops:
  0.6 42.4 %copy-start.1 = (bf16[1,512,1024]{2,1,0:T(8,128)(2,1)S(1)}, bf16[1,512,1024]{2,1,0:T(8,128)(2,1)}, u32[]{:S(2)}) copy-start(bf16[1,512,1024]{2,1,0:T(8,128)(2,1)} %param.8) | copy-start | bytes 3145732
  36.6 16.2 %collective-permute-start = (bf16[69,2,128]{0,2,1:T(8,128)(2,1)S(1)}, bf16[69,2,128]{0,2,1:T(8,128)(2,1)S(1)}, u32[]{:S(2)}, u32[]{:S(2)}) collective-permute-start(bf16[69,2,128]{0,2,1:T(8,128)(2,1)S(1)} %get-tuple-element.24), channel_id=1, source_target_pairs={{0,8},{8,16},{16,24},{24,32},{32,40},{40,48},{48,56},{56,64},{64,7... | collective-permute-start | bytes 105992 | tf_op jit(solution)/shard_map/ppermute | solution.py:25
  38.5 14.3 %collective-permute-start.1 = (bf16[69,2,128]{0,2,1:T(8,128)(2,1)S(1)}, bf16[69,2,128]{0,2,1:T(8,128)(2,1)S(1)}, u32[]{:S(2)}, u32[]{:S(2)}) collective-permute-start(bf16[69,2,128]{0,2,1:T(8,128)(2,1)S(1)} %get-tuple-element.25), channel_id=1, source_target_pairs={{8,0},{16,8},{24,16},{32,24},{40,32},{48,40},{56,48},{64,56},{72,6... | collective-permute-start | bytes 105992 | tf_op jit(solution)/shard_map/ppermute | solution.py:28
  43.3 9.4 %copy-start.5 = (s32[69]{0:T(128)S(1)}, s32[69]{0:T(128)}, u32[]{:S(2)}) copy-start(s32[69]{0:T(128)} %param.9) | copy-start | bytes 832
  44.6 25.8 %copy-start.2 = (bf16[9,256,69]{1,2,0:T(8,128)(2,1)S(1)}, bf16[9,256,69]{1,2,0:T(8,128)(2,1)}, u32[]{:S(2)}) copy-start(bf16[9,256,69]{1,2,0:T(8,128)(2,1)} %param.10) | copy-start | bytes 953860
  44.6 93.5 %all-to-all-start = ((bf16[128,1,32,128]{3,2,1,0:T(8,128)(2,1)}), bf16[128,1,32,128]{3,2,1,0:T(8,128)(2,1)}, u32[]{:S(2)}, u32[]{:S(2)}) async-start(bf16[128,1,32,128]{3,2,1,0:T(8,128)(2,1)} %bitcast.40), calls=%async_computation | async-start | bytes 2097152 | tf_op jit(solution)/shard_map/all_to_all | solution.py:53
  52.8 12.7 %collective-permute-start.3 = (bf16[69,36,2]{0,2,1:T(2,128)(2,1)S(1)}, bf16[69,36,2]{0,2,1:T(2,128)(2,1)S(1)}, u32[]{:S(2)}, u32[]{:S(2)}) collective-permute-start(bf16[69,36,2]{0,2,1:T(2,128)(2,1)S(1)} %get-tuple-element.23), channel_id=1, source_target_pairs={{1,0},{2,1},{3,2},{4,3},{5,4},{6,5},{7,6},{0,7},{9,8},{10,9},{11,1... | collective-permute-start | bytes 29816 | tf_op jit(solution)/shard_map/ppermute | solution.py:28
  58.6 11.3 %collective-permute-start.2 = (bf16[69,36,2]{0,2,1:T(2,128)(2,1)S(1)}, bf16[69,36,2]{0,2,1:T(2,128)(2,1)S(1)}, u32[]{:S(2)}, u32[]{:S(2)}) collective-permute-start(bf16[69,36,2]{0,2,1:T(2,128)(2,1)S(1)} %get-tuple-element.22), channel_id=1, source_target_pairs={{0,1},{1,2},{2,3},{3,4},{4,5},{5,6},{6,7},{7,0},{8,9},{9,10},{10,1... | collective-permute-start | bytes 29816 | tf_op jit(solution)/shard_map/ppermute | solution.py:25
  88.8 2.9 %copy-start.3 = (f32[256]{0:T(256)S(1)}, f32[256]{0:T(256)}, u32[]{:S(2)}) copy-start(f32[256]{0:T(256)} %param.11) | copy-start | bytes 3076
  91.7 12.7 %copy-start = (bf16[9,256,256]{2,1,0:T(8,128)(2,1)S(1)}, bf16[9,256,256]{2,1,0:T(8,128)(2,1)}, u32[]{:S(2)}) copy-start(bf16[9,256,256]{2,1,0:T(8,128)(2,1)} %param.12) | copy-start | bytes 3538948
  121.5 2.7 %copy-start.4 = (f32[256]{0:T(256)S(1)}, f32[256]{0:T(256)}, u32[]{:S(2)}) copy-start(f32[256]{0:T(256)} %param.13) | copy-start | bytes 3076
where the time goes:
time: 141 us
  matrix products  64.5 us (46%)
  blocking collectives  33.2 us (24%)
  starting transfers between devices  20.4 us (14%)
  waiting for transfers between devices  11.3 us (8%)
  local copies, waits for them, and re-layouts  8.31 us (6%)
  other arithmetic  2.36 us (2%)
    dot_general x18, matrix products, conv_valid(): jnp.einsum('ok,khw->ohw', weight[tap], shifted, preferred_element_type=jn...  64.5 us
    psum x5, blocking collectives, one_axis_at_a_time(): return functools.reduce(lax.psum, axes, array)  33.2 us
    ppermute x2, starting transfers between devices, padded_2(): lax.ppermute(lax.slice_in_dim(block, 0, width, axis=dim), axis, backward)  10.3 us
    all_to_all x1, starting transfers between devices, regrid(): lax.all_to_all(ordered, LAT_LON, split_axis=0, concat_axis=1, tiled=True)  8.12 us
    ppermute x2, waiting for transfers between devices, padded_2(): lax.ppermute(lax.slice_in_dim(block, 0, width, axis=dim), axis, backward)  6.94 us
    unnamed x15, local copies, waits for them, and re-layouts  5.21 us
    ppermute x2, waiting for transfers between devices, padded_2(): lax.ppermute(lax.slice_in_dim(block, block.shape[dim] - width, None, axis...  4.35 us
  transfers between devices with their start and end apart: 5, of which 2 were waited for; matrix products, arithmetic and copies ran while one was open for 49% of the time, Pallas kernels for 0%

commit v1 on v0

v1 whole, which is shorter than its diff:
```python
import functools
import random

import jax
import jax.numpy as jnp
from jax import lax
from jax.experimental import pallas as pl
from jax.experimental.pallas import tpu as pltpu
from jax.sharding import PartitionSpec as P

MESH = pl.DeviceIdType.MESH
KB = 80
KP = 256


def gelu(v):
    u = v * (0.7978845608028654 + 0.035677408136300125 * (v * v))
    half = 0.5 * v
    return half + half * jnp.tanh(u)


def kernel(n_lat, n_lon, channels, rows, cols, hid_ch,
           cur_hbm, nf_hbm, slot_hbm, w1_hbm, b1_hbm, w2_hbm, b2_hbm,
           feat_ref, next_ref,
           cur, w1, w2, bv, slot, tt, aa, sa, xx, xe, w1c, w1s, bias, hid, edge,
           stat, srecv, recv, in_sem, h_send, h_recv, s_send, s_recv, a_send, a_recv):
    f32, bf16 = jnp.float32, jnp.bfloat16
    n_dev = n_lat * n_lon
    lat = lax.axis_index("lat")
    lon = lax.axis_index("lon")
    me = lat * n_lon + lon
    la = [lax.rem(lat + d, n_lat) for d in range(n_lat)]
    lo = [lax.rem(lon + d, n_lon) for d in range(n_lon)]
    order = [(a, b) for a in range(n_lat) for b in range(n_lon) if (a, b) != (0, 0)]
    random.Random(0).shuffle(order)

    def load(i, src, dst):
        return pltpu.make_async_copy(src, dst, in_sem.at[i])

    loads = [load(0, cur_hbm, cur), load(1, w1_hbm, w1), load(2, b1_hbm, bv.at[0]),
             load(3, b2_hbm, bv.at[1]), load(4, w2_hbm, w2), load(5, slot_hbm, slot)]
    for c in loads:
        c.start()
    own = pltpu.make_async_copy(
        nf_hbm.at[0, pl.ds(pl.multiple_of(lat * rows, rows), rows), pl.ds(pl.multiple_of(lon * cols, cols), cols)],
        recv.at[me], in_sem.at[6])
    own.start()
    barrier = pltpu.get_barrier_semaphore()
    for a, b in order:
        pl.semaphore_signal(barrier, inc=1, device_id=(la[a], lo[b]), device_id_type=MESH)

    tt[2:rows + 2, 64:KB, :] = jnp.zeros((rows, KB - 64, cols), bf16)
    loads[0].wait()
    sum1 = jnp.zeros((channels, cols), f32)
    sum2 = jnp.zeros((channels, cols), f32)
    for h in range(0, rows, 8):
        t = jnp.swapaxes(cur[:, h:h + 8, :].astype(f32), 0, 1)
        sum1 = sum1 + jnp.sum(t, axis=0)
        sum2 = sum2 + jnp.sum(t * t, axis=0)
        tt[2 + h:10 + h, 0:channels, :] = t.astype(bf16)
    diag = lax.broadcasted_iota(jnp.int32, (channels, cols), 0) == lax.broadcasted_iota(jnp.int32, (channels, cols), 1)
    for i, s in enumerate((sum1, sum2)):
        col = jnp.sum(s, axis=1, keepdims=True)
        stat[i:i + 1, :] = jnp.sum(jnp.where(diag, col, 0.0), axis=0, keepdims=True)
    lane = lax.broadcasted_iota(jnp.int32, (KB, cols), 1)
    lane_row = lax.shift_right_logical(lane * 171, 9)
    lane_col = lane - 3 * lane_row

    def strips(first, last, base):
        out = list(base)
        for r in range(first, last):
            v = tt[r]
            for s in range(2):
                out[s] = jnp.where(lane_row == r, pltpu.roll(v, (3 * r + 2 - s) % cols, axis=1), out[s])
        return out

    zero = jnp.zeros((KB, cols), bf16)
    strip = strips(2, rows + 2, (zero, zero))
    aa[0] = strip[0]
    aa[1] = strip[1]
    loads[1].wait()
    w1c[...] = jnp.zeros_like(w1c)
    for tap in range(9):
        w1c[tap // 3, :, KB * (tap % 3):KB * (tap % 3) + channels] = w1[tap]
    xx[:, 3 * KB:KP, :] = jnp.zeros((rows + 4, KP - 3 * KB, cols), bf16)
    xe[:, :, 3 * KB:KP, :] = jnp.zeros((3, 2, KP - 3 * KB, cols), bf16)
    loads[2].wait()
    loads[3].wait()
    eye = lax.broadcasted_iota(jnp.int32, (hid_ch, hid_ch), 0) == lax.broadcasted_iota(jnp.int32, (hid_ch, hid_ch), 1)
    for i in range(2):
        col = jnp.sum(jnp.where(eye, bv[i], 0.0), axis=1, keepdims=True)
        bias[i] = jnp.broadcast_to(col, (hid_ch, cols))
    srecv[me] = stat[...]
    pl.semaphore_wait(barrier, n_dev - 1)

    up, down, east, west = la[n_lat - 1], la[1], lo[1], lo[n_lon - 1]
    halo = [
        (aa.at[0], sa.at[0], lat, east), (aa.at[0], sa.at[1], up, east), (aa.at[0], sa.at[2], down, east),
        (aa.at[1], sa.at[3], lat, west), (aa.at[1], sa.at[4], up, west), (aa.at[1], sa.at[5], down, west),
        (tt.at[pl.ds(2, 2)], tt.at[pl.ds(rows + 2, 2)], up, lon), (tt.at[pl.ds(rows, 2)], tt.at[pl.ds(0, 2)], down, lon),
    ]
    sent = []
    for i, (src, dst, p, q) in enumerate(halo):
        c = pltpu.make_async_remote_copy(src, dst, h_send.at[i], h_recv.at[i], device_id=(p, q), device_id_type=MESH)
        c.start()
        sent.append(c)
    for a, b in order:
        pltpu.make_async_remote_copy(stat, srecv.at[me], s_send, s_recv,
                                     device_id=(la[a], lo[b]), device_id_type=MESH).start()
    for a, b in order:
        pltpu.make_async_remote_copy(
            nf_hbm.at[0, pl.ds(pl.multiple_of(la[a] * rows, rows), rows), pl.ds(pl.multiple_of(lo[b] * cols, cols), cols)],
            recv.at[me], a_send, a_recv, device_id=(la[a], lo[b]), device_id_type=MESH).start()

    for c in sent:
        c.wait_recv()
    first = lat == 0
    last = lat == n_lat - 1
    for r in (0, 1):
        tt[r] = jnp.where(first, zero, tt[r])
        tt[rows + 2 + r] = jnp.where(last, zero, tt[rows + 2 + r])
    strip = strips(0, 2, strips(rows + 2, rows + 4, (aa[0], aa[1])))
    valid = (lane < 3 * (rows + 4)) & ((lane >= 6) | (lat > 0)) & ((lane < 3 * (rows + 2)) | (lat < n_lat - 1))
    shift = 3 * rows
    west_in = jnp.where(lane < 6, pltpu.roll(sa[2], cols - shift, axis=1),
                        jnp.where(lane < 3 * (rows + 2), sa[0], pltpu.roll(sa[1], shift, axis=1)))
    east_in = jnp.where(lane < 6, pltpu.roll(sa[5], cols - shift, axis=1),
                        jnp.where(lane < 3 * (rows + 2), sa[3], pltpu.roll(sa[4], shift, axis=1)))
    g_west = jnp.where(valid, jnp.where(lane_col == 2, strip[0], west_in), zero)
    g_east = jnp.where(valid, jnp.where(lane_col == 0, strip[1], east_in), zero)
    for a in range(3):
        for b in range(3):
            amount = (-(3 * (a - 1) + b - 1)) % cols
            for s, g in enumerate((g_west, g_east)):
                xe[a, s, KB * b:KB * (b + 1), :] = pltpu.roll(g, amount, axis=1) if amount else g
    for r in range(rows + 4):
        v = tt[r]
        center = 3 * r + 1
        xx[r, 0:KB, :] = jnp.where(lane == 0, pltpu.roll(g_west, (-center) % cols, axis=1), pltpu.roll(v, 1, axis=1))
        xx[r, KB:2 * KB, :] = v
        xx[r, 2 * KB:3 * KB, :] = jnp.where(
            lane == cols - 1, pltpu.roll(g_east, (cols - 1 - center) % cols, axis=1), pltpu.roll(v, cols - 1, axis=1))

    def drain(buf, sem):
        w = buf.at[pl.ds(0, n_dev - 1)]
        pltpu.make_async_copy(w, w, sem).wait()

    drain(srecv, s_recv)
    total = jnp.sum(srecv[...], axis=0) / (n_dev * rows * cols)
    mean = total[0:1, :]
    scale = 1.0 / jnp.sqrt(total[1:2, :] - mean * mean + 1e-05)
    in_use = lax.broadcasted_iota(jnp.int32, (1, cols), 1) < channels

    def beside(v):
        wide = jnp.concatenate([jnp.where(in_use, v, 0.0), jnp.zeros((1, KP - cols), f32)], axis=1)
        return wide + pltpu.roll(wide, KB, axis=1) + pltpu.roll(wide, 2 * KB, axis=1)

    mean_k, scale_k = beside(mean), beside(scale)
    full = bias[0]
    for a in range(3):
        ws = (w1c[a].astype(f32) * scale_k).astype(bf16)
        w1s[a] = ws
        part = jnp.broadcast_to(jnp.sum(ws.astype(f32) * mean_k, axis=1, keepdims=True), (hid_ch, cols))
        full = full - part
        if a != 1:
            bias[2 + a // 2] = part
    bias[0] = full

    top = jnp.where(first, 1.0, 0.0).astype(f32)
    bottom = jnp.where(last, 1.0, 0.0).astype(f32)
    hlane = lax.broadcasted_iota(jnp.int32, (hid_ch, cols), 1)

    def conv1(parts):
        acc = jnp.zeros((hid_ch, cols * len(parts(0))), f32)
        for a in range(3):
            acc = acc + jnp.dot(w1s[a], jnp.concatenate(parts(a), axis=1), preferred_element_type=f32)
        return acc

    def put(r, h):
        hid[1, r] = h
        center = 3 * (r + 1) + 1
        hid[0, r] = jnp.where(hlane == 0, pltpu.roll(edge[0], lax.rem(2 * cols - center, cols), axis=1), pltpu.roll(h, 1, axis=1))
        hid[2, r] = jnp.where(hlane == cols - 1, pltpu.roll(edge[1], lax.rem(2 * cols - 1 - center, cols), axis=1),
                              pltpu.roll(h, cols - 1, axis=1))

    acc = conv1(lambda a: [xe[a, 0], xe[a, 1], xx[rows + a], xx[rows + 1 + a]])
    ebias = (bias[0] + jnp.where((hlane >= 6) & (hlane < 9), top, 0.0) * bias[2]
             + jnp.where((hlane >= 3 * rows + 3) & (hlane < 3 * rows + 6), bottom, 0.0) * bias[3])
    keep = (((hlane >= 6) | (lat > 0)) & ((hlane < 3 * rows + 6) | (lat < n_lat - 1)))
    for s in range(2):
        edge[s] = jnp.where(keep, gelu(acc[:, s * cols:(s + 1) * cols] + ebias), 0.0).astype(bf16)
    put(rows, gelu(acc[:, 2 * cols:3 * cols] + (bias[0] + bottom * bias[3])).astype(bf16))
    put(rows + 1, jnp.where(last, 0.0, gelu(acc[:, 3 * cols:] + bias[0])).astype(bf16))

    def tile1(r0):
        acc = conv1(lambda a: [xx[r0 + a + q] for q in range(4)])
        for q in range(4):
            v = acc[:, q * cols:(q + 1) * cols] + bias[0]
            if r0 == 0 and q == 1:
                v = v + top * bias[2]
            h = gelu(v)
            if r0 == 0 and q == 0:
                h = jnp.where(first, 0.0, h)
            put(r0 + q, h.astype(bf16))

    def tile2(r0):
        acc = jnp.zeros((hid_ch, 4 * cols), f32)
        for a in range(3):
            for b in range(3):
                x = jnp.concatenate([hid[b, r0 + a + q] for q in range(4)], axis=1)
                acc = acc + jnp.dot(w2[3 * a + b], x, preferred_element_type=f32)
        return [acc[:, q * cols:(q + 1) * cols] + bias[1] for q in range(4)]

    loads[4].wait()
    for r0 in (0, 4, 8):
        tile1(r0)
    for g in range(rows // 8):
        for r0 in (8 * g + 12, 8 * g + 16):
            if r0 < rows:
                tile1(r0)
        outs = tile2(8 * g) + tile2(8 * g + 4)
        feat_ref[:, 8 * g:8 * g + 8, :] = jnp.swapaxes(jnp.stack(outs, axis=0), 0, 1).astype(bf16)

    own.wait()
    loads[5].wait()
    drain(recv, a_recv)
    for c in range(channels):
        next_ref[c] = recv[slot[c]]
    for c in sent:
        c.wait_send()
    drain(srecv, s_send)
    drain(recv, a_send)


def solution(mesh):
    n_lat, n_lon = mesh.shape["lat"], mesh.shape["lon"]
    n_dev = n_lat * n_lon

    def body(current, next_fields, reader_slot, first_weight, first_bias, second_weight, second_bias):
        channels, rows, cols = current.shape
        hid_ch = first_weight.shape[1]
        bf16, f32 = jnp.bfloat16, jnp.float32
        dma = pltpu.SemaphoreType.DMA
        return pl.pallas_call(
            functools.partial(kernel, n_lat, n_lon, channels, rows, cols, hid_ch),
            out_shape=(jax.ShapeDtypeStruct((hid_ch, rows, cols), bf16), jax.ShapeDtypeStruct((channels, rows, cols), bf16)),
            in_specs=[pl.BlockSpec(memory_space=pl.ANY)] * 7,
            out_specs=(pl.BlockSpec(memory_space=pltpu.VMEM),) * 2,
            scratch_shapes=[
                pltpu.VMEM((channels, rows, cols), bf16),
                pltpu.VMEM(first_weight.shape, bf16),
                pltpu.VMEM(second_weight.shape, bf16),
                pltpu.VMEM((2, 1, hid_ch), f32),
                pltpu.SMEM(reader_slot.shape, jnp.int32),
                pltpu.VMEM((rows + 4, KB, cols), bf16),
                pltpu.VMEM((2, KB, cols), bf16),
                pltpu.VMEM((6, KB, cols), bf16),
                pltpu.VMEM((rows + 4, KP, cols), bf16),
                pltpu.VMEM((3, 2, KP, cols), bf16),
                pltpu.VMEM((3, hid_ch, KP), bf16),
                pltpu.VMEM((3, hid_ch, KP), bf16),
                pltpu.VMEM((4, hid_ch, cols), f32),
                pltpu.VMEM((3, rows + 2, hid_ch, cols), bf16),
                pltpu.VMEM((2, hid_ch, cols), bf16),
                pltpu.VMEM((2, cols), f32),
                pltpu.VMEM((n_dev, 2, cols), f32),
                pltpu.VMEM((n_dev, rows, cols), bf16),
                dma((7,)), dma((8,)), dma((8,)), dma, dma, dma, dma,
            ],
            compiler_params=pltpu.CompilerParams(collective_id=0, has_side_effects=True, vmem_limit_bytes=40 * 1024 * 1024),
        )(current, next_fields, reader_slot, first_weight, first_bias.reshape(1, -1), second_weight, second_bias.reshape(1, -1))

    split = P(None, "lat", "lon")
    return jax.shard_map(
        body,
        mesh=mesh,
        in_specs=(split, P(("lat", "lon"), None, None), P(), P(), P(), P(), P()),
        out_specs=(split, split),
        check_vma=False,
    )
```

time: 141 us -> 47.4 us (0.34)
  the two profiles are of different devices: /device:TPU:4 before, /device:TPU:1 now
where the time goes in v1:
time: 47.4 us; the launch traced here: 47.1 us
  Pallas kernels  37.5 us (79%)
  local copies, waits for them, and re-layouts  8.99 us (19%)
  between operations  0.65 us (1%)
    pallas_call x1, Pallas kernels, body(): pl.pallas_call(functools.partial(kernel, n_lat, n_lon, channels, rows, co...  37.5 us
    unnamed x15, local copies, waits for them, and re-layouts  8.99 us

profile of v1, /device:TPU:1, one launch (start us, length us, event | category | flops | bytes accessed | tf_op | source)
XLA Modules:
  0.0 47.1 jit_solution(11138006345916530156)
XLA Ops:
  0.6 1.3 %copy.9.w1_hbm = bf16[9,256,69]{2,1,0:T(8,128)(2,1)S(1)} copy(bf16[9,256,69]{1,2,0:T(8,128)(2,1)} %param.10) | data formatting | bytes 635904 | tf_op args[3]
  1.9 0.0 copy-start
  1.9 1.3 %copy-done = bf16[9,256,256]{2,1,0:T(8,128)(2,1)S(1)} copy-done((bf16[9,256,256]{2,1,0:T(8,128)(2,1)S(1)}, bf16[9,256,256]{2,1,0:T(8,128)(2,1)}, u32[]{:S(2)}) %copy-start) | copy-done | bytes 1179672
  3.2 0.0 copy-start.1
  3.2 1.2 %copy-done.1 = bf16[1,512,1024]{2,1,0:T(8,128)(2,1)S(1)} copy-done((bf16[1,512,1024]{2,1,0:T(8,128)(2,1)S(1)}, bf16[1,512,1024]{2,1,0:T(8,128)(2,1)}, u32[]{:S(2)}) %copy-start.1) | copy-done | bytes 1048600
  4.4 0.0 copy-start.2
  4.4 1.1 %copy-done.2 = bf16[69,32,128]{2,1,0:T(8,128)(2,1)S(1)} copy-done((bf16[69,32,128]{2,1,0:T(8,128)(2,1)S(1)}, bf16[69,32,128]{2,1,0:T(8,128)(2,1)}, u32[]{:S(2)}) %copy-start.2) | copy-done | bytes 565272
  5.5 0.0 copy-start.3
  5.5 0.7 %copy-done.3 = f32[256]{0:T(256)S(1)} copy-done((f32[256]{0:T(256)S(1)}, f32[256]{0:T(256)}, u32[]{:S(2)}) %copy-start.3) | copy-done | bytes 1048
  6.2 0.0 copy-start.4
  6.2 0.7 %copy-done.4 = f32[256]{0:T(256)S(1)} copy-done((f32[256]{0:T(256)S(1)}, f32[256]{0:T(256)}, u32[]{:S(2)}) %copy-start.4) | copy-done | bytes 1048
  6.8 0.0 copy-start.5
  6.9 0.7 %copy-done.5 = s32[69]{0:T(128)S(1)} copy-done((s32[69]{0:T(128)S(1)}, s32[69]{0:T(128)}, u32[]{:S(2)}) %copy-start.5) | copy-done | bytes 300
  7.5 37.5 %shard_map.86 = (bf16[256,32,128]{2,1,0:T(8,128)(2,1)S(1)}, bf16[69,32,128]{2,1,0:T(8,128)(2,1)S(1)}) custom-call(bf16[69,32,128]{2,1,0:T(8,128)(2,1)S(1)} %copy-done.2, bf16[1,512,1024]{2,1,0:T(8,128)(2,1)S(1)} %copy-done.1, s32[69]{0:T(128)S(1)} %copy-done.5, bf16[9,256,69]{2,1,0:T(8,128)(2,1)S(1)} %copy.9.w1_hbm, f32[1,256]{1,0:T(1,128)S(1)} %bitcast.2, ...), custom_call_target="tpu_custom_call" | custom-call | tf_op jit(solution)/shard_map/pallas_call | solution.py:244
  45.0 1.3 %copy.12 = bf16[256,32,128]{2,1,0:T(8,128)(2,1)} copy(bf16[256,32,128]{2,1,0:T(8,128)(2,1)S(1)} %get-tuple-element.4) | data formatting | bytes 4194304
  46.3 0.8 %copy.13 = bf16[69,32,128]{2,1,0:T(8,128)(2,1)} copy(bf16[69,32,128]{2,1,0:T(8,128)(2,1)S(1)} %get-tuple-element.5) | data formatting | bytes 1130496
Async XLA Ops:
  1.9 1.3 %copy-start = (bf16[9,256,256]{2,1,0:T(8,128)(2,1)S(1)}, bf16[9,256,256]{2,1,0:T(8,128)(2,1)}, u32[]{:S(2)}) copy-start(bf16[9,256,256]{2,1,0:T(8,128)(2,1)} %w2_hbm.1) | copy-start | bytes 3538948
  3.2 1.2 %copy-start.1 = (bf16[1,512,1024]{2,1,0:T(8,128)(2,1)S(1)}, bf16[1,512,1024]{2,1,0:T(8,128)(2,1)}, u32[]{:S(2)}) copy-start(bf16[1,512,1024]{2,1,0:T(8,128)(2,1)} %nf_hbm.1) | copy-start | bytes 3145732
  4.4 1.1 %copy-start.2 = (bf16[69,32,128]{2,1,0:T(8,128)(2,1)S(1)}, bf16[69,32,128]{2,1,0:T(8,128)(2,1)}, u32[]{:S(2)}) copy-start(bf16[69,32,128]{2,1,0:T(8,128)(2,1)} %cur_hbm.1) | copy-start | bytes 1695748
  5.5 0.7 %copy-start.3 = (f32[256]{0:T(256)S(1)}, f32[256]{0:T(256)}, u32[]{:S(2)}) copy-start(f32[256]{0:T(256)} %param.11) | copy-start | bytes 3076
  6.2 0.7 %copy-start.4 = (f32[256]{0:T(256)S(1)}, f32[256]{0:T(256)}, u32[]{:S(2)}) copy-start(f32[256]{0:T(256)} %param.13) | copy-start | bytes 3076
  6.8 0.7 %copy-start.5 = (s32[69]{0:T(128)S(1)}, s32[69]{0:T(128)}, u32[]{:S(2)}) copy-start(s32[69]{0:T(128)} %slot_hbm.1) | copy-start | bytes 832

commit v2 on v1

--- a/solution.py
+++ b/solution.py
@@ -81,7 +81,9 @@
     loads[1].wait()
     w1c[...] = jnp.zeros_like(w1c)
     for tap in range(9):
-        w1c[tap // 3, :, KB * (tap % 3):KB * (tap % 3) + channels] = w1[tap]
+        w1c[tap // 3, KB * (tap % 3):KB * (tap % 3) + channels, :] = w1[tap]
+    for a in range(3):
+        w1c[a] = jnp.transpose(w1c[a])
     xx[:, 3 * KB:KP, :] = jnp.zeros((rows + 4, KP - 3 * KB, cols), bf16)
     xe[:, :, 3 * KB:KP, :] = jnp.zeros((3, 2, KP - 3 * KB, cols), bf16)
     loads[2].wait()
@@ -244,11 +246,11 @@
         return pl.pallas_call(
             functools.partial(kernel, n_lat, n_lon, channels, rows, cols, hid_ch),
             out_shape=(jax.ShapeDtypeStruct((hid_ch, rows, cols), bf16), jax.ShapeDtypeStruct((channels, rows, cols), bf16)),
-            in_specs=[pl.BlockSpec(memory_space=pl.ANY)] * 7,
+            in_specs=[pl.BlockSpec(memory_space=pltpu.HBM)] * 7,
             out_specs=(pl.BlockSpec(memory_space=pltpu.VMEM),) * 2,
             scratch_shapes=[
                 pltpu.VMEM((channels, rows, cols), bf16),
-                pltpu.VMEM(first_weight.shape, bf16),
+                pltpu.VMEM((9, channels, hid_ch), bf16),
                 pltpu.VMEM(second_weight.shape, bf16),
                 pltpu.VMEM((2, 1, hid_ch), f32),
                 pltpu.SMEM(reader_slot.shape, jnp.int32),
@@ -257,7 +259,7 @@
                 pltpu.VMEM((6, KB, cols), bf16),
                 pltpu.VMEM((rows + 4, KP, cols), bf16),
                 pltpu.VMEM((3, 2, KP, cols), bf16),
-                pltpu.VMEM((3, hid_ch, KP), bf16),
+                pltpu.VMEM((3, KP, hid_ch), bf16),
                 pltpu.VMEM((3, hid_ch, KP), bf16),
                 pltpu.VMEM((4, hid_ch, cols), f32),
                 pltpu.VMEM((3, rows + 2, hid_ch, cols), bf16),
@@ -268,7 +270,9 @@
                 dma((7,)), dma((8,)), dma((8,)), dma, dma, dma, dma,
             ],
             compiler_params=pltpu.CompilerParams(collective_id=0, has_side_effects=True, vmem_limit_bytes=40 * 1024 * 1024),
-        )(current, next_fields, reader_slot, first_weight, first_bias.reshape(1, -1), second_weight, second_bias.reshape(1, -1))
+        )(*(pltpu.with_memory_space_constraint(v, pltpu.HBM) for v in (
+            current, next_fields, reader_slot, jnp.swapaxes(first_weight, 1, 2), first_bias.reshape(1, -1),
+            second_weight, second_bias.reshape(1, -1))))
 
     split = P(None, "lat", "lon")
     return jax.shard_map(

time: 47.4 us -> 40 us (0.84)
  local copies, waits for them, and re-layouts: 8.99 us -> 2.13 us
    unnamed x15 -> x2, local copies, waits for them, and re-layouts: 8.99 us -> 2.13 us
where the time goes in v2:
time: 40 us; the launch traced here: 39.9 us
  Pallas kernels  37.1 us (93%)
  local copies, waits for them, and re-layouts  2.13 us (5%)
  between operations  0.64 us (2%)
    pallas_call x1, Pallas kernels, body(): pl.pallas_call(functools.partial(kernel, n_lat, n_lon, channels, rows, co...  37.1 us
    unnamed x2, local copies, waits for them, and re-layouts  2.13 us

profile of v2, /device:TPU:1, one launch (start us, length us, event | category | flops | bytes accessed | tf_op | source)
XLA Modules:
  0.0 39.9 jit_solution(5135132254668322871)
XLA Ops:
  0.6 37.1 %shard_map.86 = (bf16[256,32,128]{2,1,0:T(8,128)(2,1)S(1)}, bf16[69,32,128]{2,1,0:T(8,128)(2,1)S(1)}) custom-call(bf16[69,32,128]{2,1,0:T(8,128)(2,1)} %cur_hbm.1, bf16[1,512,1024]{2,1,0:T(8,128)(2,1)} %nf_hbm.1, s32[69]{0:T(128)} %slot_hbm.1, bf16[9,69,256]{2,1,0:T(8,128)(2,1)} %bitcast.3, f32[1,256]{1,0:T(1,128)} %bitcast.4, bf16[9,256,256]{2,1,0:T(8,128)(2,1)} %w2_hbm.1, ...), custom_call_target="tpu_custom_call" | custom-call | tf_op jit(solution)/shard_map/pallas_call | solution.py:246
  37.8 1.3 %copy.11 = bf16[256,32,128]{2,1,0:T(8,128)(2,1)} copy(bf16[256,32,128]{2,1,0:T(8,128)(2,1)S(1)} %get-tuple-element.4) | data formatting | bytes 4194304
  39.1 0.8 %copy.12 = bf16[69,32,128]{2,1,0:T(8,128)(2,1)} copy(bf16[69,32,128]{2,1,0:T(8,128)(2,1)S(1)} %get-tuple-element.5) | data formatting | bytes 1130496

commit v3 on v2

--- a/solution.py
+++ b/solution.py
@@ -78,6 +78,24 @@
     strip = strips(2, rows + 2, (zero, zero))
     aa[0] = strip[0]
     aa[1] = strip[1]
+    srecv[me] = stat[...]
+    pl.semaphore_wait(barrier, n_dev - 1)
+
+    for a, b in order:
+        pltpu.make_async_remote_copy(stat, srecv.at[me], s_send, s_recv,
+                                     device_id=(la[a], lo[b]), device_id_type=MESH).start()
+    up, down, east, west = la[n_lat - 1], la[1], lo[1], lo[n_lon - 1]
+    halo = [
+        (aa.at[0], sa.at[0], lat, east), (aa.at[0], sa.at[1], up, east), (aa.at[0], sa.at[2], down, east),
+        (aa.at[1], sa.at[3], lat, west), (aa.at[1], sa.at[4], up, west), (aa.at[1], sa.at[5], down, west),
+        (tt.at[pl.ds(2, 2)], tt.at[pl.ds(rows + 2, 2)], up, lon), (tt.at[pl.ds(rows, 2)], tt.at[pl.ds(0, 2)], down, lon),
+    ]
+    sent = []
+    for i, (src, dst, p, q) in enumerate(halo):
+        c = pltpu.make_async_remote_copy(src, dst, h_send.at[i], h_recv.at[i], device_id=(p, q), device_id_type=MESH)
+        c.start()
+        sent.append(c)
+
     loads[1].wait()
     w1c[...] = jnp.zeros_like(w1c)
     for tap in range(9):
@@ -92,30 +110,14 @@
     for i in range(2):
         col = jnp.sum(jnp.where(eye, bv[i], 0.0), axis=1, keepdims=True)
         bias[i] = jnp.broadcast_to(col, (hid_ch, cols))
-    srecv[me] = stat[...]
-    pl.semaphore_wait(barrier, n_dev - 1)
-
-    up, down, east, west = la[n_lat - 1], la[1], lo[1], lo[n_lon - 1]
-    halo = [
-        (aa.at[0], sa.at[0], lat, east), (aa.at[0], sa.at[1], up, east), (aa.at[0], sa.at[2], down, east),
-        (aa.at[1], sa.at[3], lat, west), (aa.at[1], sa.at[4], up, west), (aa.at[1], sa.at[5], down, west),
-        (tt.at[pl.ds(2, 2)], tt.at[pl.ds(rows + 2, 2)], up, lon), (tt.at[pl.ds(rows, 2)], tt.at[pl.ds(0, 2)], down, lon),
-    ]
-    sent = []
-    for i, (src, dst, p, q) in enumerate(halo):
-        c = pltpu.make_async_remote_copy(src, dst, h_send.at[i], h_recv.at[i], device_id=(p, q), device_id_type=MESH)
-        c.start()
-        sent.append(c)
-    for a, b in order:
-        pltpu.make_async_remote_copy(stat, srecv.at[me], s_send, s_recv,
-                                     device_id=(la[a], lo[b]), device_id_type=MESH).start()
+
+    for c in sent:
+        c.wait_recv()
     for a, b in order:
         pltpu.make_async_remote_copy(
             nf_hbm.at[0, pl.ds(pl.multiple_of(la[a] * rows, rows), rows), pl.ds(pl.multiple_of(lo[b] * cols, cols), cols)],
             recv.at[me], a_send, a_recv, device_id=(la[a], lo[b]), device_id_type=MESH).start()
 
-    for c in sent:
-        c.wait_recv()
     first = lat == 0
     last = lat == n_lat - 1
     for r in (0, 1):

time: 40 us -> 35.3 us (0.88)
  the two profiles are of different devices: /device:TPU:1 before, /device:TPU:8 now
where the time goes in v3:
time: 35.3 us; the launch traced here: 35.2 us
  Pallas kernels  32.4 us (92%)
  local copies, waits for them, and re-layouts  2.13 us (6%)
  between operations  0.64 us (2%)
    pallas_call x1, Pallas kernels, body(): pl.pallas_call(functools.partial(kernel, n_lat, n_lon, channels, rows, co...  32.4 us
    unnamed x2, local copies, waits for them, and re-layouts  2.13 us

profile of v3, /device:TPU:8, one launch (start us, length us, event | category | flops | bytes accessed | tf_op | source)
XLA Modules:
  0.0 35.2 jit_solution(4071568096132810064)
XLA Ops:
  0.6 32.4 %shard_map.86 = (bf16[256,32,128]{2,1,0:T(8,128)(2,1)S(1)}, bf16[69,32,128]{2,1,0:T(8,128)(2,1)S(1)}) custom-call(bf16[69,32,128]{2,1,0:T(8,128)(2,1)} %cur_hbm.1, bf16[1,512,1024]{2,1,0:T(8,128)(2,1)} %nf_hbm.1, s32[69]{0:T(128)} %slot_hbm.1, bf16[9,69,256]{2,1,0:T(8,128)(2,1)} %bitcast.3, f32[1,256]{1,0:T(1,128)} %bitcast.4, bf16[9,256,256]{2,1,0:T(8,128)(2,1)} %w2_hbm.1, ...), custom_call_target="tpu_custom_call" | custom-call | tf_op jit(solution)/shard_map/pallas_call | solution.py:248
  33.0 1.3 %copy.11 = bf16[256,32,128]{2,1,0:T(8,128)(2,1)} copy(bf16[256,32,128]{2,1,0:T(8,128)(2,1)S(1)} %get-tuple-element.4) | data formatting | bytes 4194304
  34.4 0.8 %copy.12 = bf16[69,32,128]{2,1,0:T(8,128)(2,1)} copy(bf16[69,32,128]{2,1,0:T(8,128)(2,1)S(1)} %get-tuple-element.5) | data formatting | bytes 1130496
